TPU v7x, 256 devices: a whole 4x4x8 slice. The times are simulated.
256 devices in a mesh: gx: 16 (over z_lo, x), gy: 4 (over y), gz: 4 (over z_hi, core).
Axes of the slice: x: 4, y: 4, z: 8 (z_hi: 2, z_lo: 4; z = z_hi * 4 + z_lo), core: 2. Of those that a mesh axis runs over, the one named last changes fastest.
Arguments:
- tokens: bfloat16 [8192, 4608], P('gx', 'gy'), may hold values from -6 to 6
- base_up_weight: bfloat16 [4608, 18432], P('gy', ('gz', 'gx')), may hold values from -0.09375 to 0.09375
- adapter_down_weight: bfloat16 [64, 16, 4608], P(None, None, 'gy'), may hold values from -0.09375 to 0.09375
- adapter_up_weight: bfloat16 [64, 16, 18432], P('gx', None, 'gz'), may hold values from -1.5 to 1.5
- block_adapter_index: int32 [64], P('gx'), may hold values from 0 to 63
- request_rows: int32 [64], P('gx'), may hold values from 1 to 128
Outputs:
- projected: bfloat16 [8192, 18432], P(('gx', 'gy'), 'gz')
Inputs may be any that keep to these rules, and one draw needn't show every extreme that they name: `request_rows`: live rows of each block.
All inputs are finite; a program needn't handle non-finite values.
Results may differ from a plain program's by a relative error of at most 0.0047.
Values may be sent and summed in bfloat16 or wider, within the bound.
A program may use at most 128 MiB of HBM per device.

v0:
```python
import jax
import jax.numpy as jnp
from jax import lax
from jax.sharding import PartitionSpec as P

ADAPTER_COUNT = 64
BLOCK = 128


def sent_to_all(array, axis):
    size = lax.axis_size(axis)
    return lax.all_to_all(
        jnp.broadcast_to(array[None], (size, *array.shape)), axis, 0, 0, tiled=True
    )


def taken_together(array, axis):
    return sent_to_all(array, axis).sum(axis=0)


def in_blocks(array, dim, size):
    before, after = (array.shape[:dim], array.shape[dim + 1 :])
    return jnp.moveaxis(array.reshape(*before, size, -1, *after), dim, 0)


def summed_on_arrival(array, axis, dim):
    size = lax.axis_size(axis)
    tiles = lax.all_to_all(in_blocks(array, dim, size), axis, 0, 0, tiled=True)
    return jnp.sum(tiles.astype(jnp.float32), axis=0)


def body(
    tokens,
    base_up_weight,
    adapter_down_weight,
    adapter_up_weight,
    block_adapter_index,
    request_rows,
):
    rows, shard_width = tokens.shape
    groups = lax.axis_size("gy")
    blocks = rows // BLOCK
    own_blocks = blocks // groups
    own_rows = own_blocks * BLOCK
    first = lax.axis_index("gy") * own_blocks
    rank_values = adapter_down_weight.shape[1]
    catalog = jnp.arange(ADAPTER_COUNT, dtype=jnp.int32)
    selected_adapters = (block_adapter_index[:, None] == catalog[None, :]).astype(jnp.bfloat16)
    chosen_down = jnp.dot(
        selected_adapters,
        adapter_down_weight.reshape(ADAPTER_COUNT, rank_values * shard_width),
        preferred_element_type=jnp.float32,
    )
    chosen_down = chosen_down.astype(jnp.bfloat16).reshape(blocks, rank_values, shard_width)
    tok_blocks = tokens.reshape(blocks, BLOCK, shard_width)
    shrink_part = jnp.einsum(
        "bmd,brd->bmr", tok_blocks, chosen_down, preferred_element_type=jnp.float32
    )
    shrink_all = taken_together(shrink_part, "gy")
    shrink_own = lax.dynamic_slice_in_dim(shrink_all, first, own_blocks, 0)
    shrink_low = shrink_own.astype(jnp.bfloat16)
    adapter_factors = lax.all_gather(adapter_up_weight, "gx", axis=0, tiled=True)
    out_width = adapter_factors.shape[2]
    own_picks = lax.dynamic_slice_in_dim(selected_adapters, first, own_blocks, 0)
    chosen_up = jnp.dot(
        own_picks,
        adapter_factors.reshape(ADAPTER_COUNT, rank_values * out_width),
        preferred_element_type=jnp.float32,
    )
    chosen_up = chosen_up.astype(jnp.bfloat16).reshape(own_blocks, rank_values, out_width)
    expand = jnp.einsum("bmr,brf->bmf", shrink_low, chosen_up, preferred_element_type=jnp.float32)
    expand = expand.reshape(own_rows, out_width)
    partial_value = jnp.dot(
        tokens,
        lax.all_gather(base_up_weight, "gx", axis=1, tiled=True),
        preferred_element_type=jnp.float32,
    )
    extra = 2.0 * expand
    total = summed_on_arrival(partial_value.astype(jnp.bfloat16), "gy", 0) + extra
    own_live = lax.dynamic_slice_in_dim(request_rows, first, own_blocks, 0)
    live_mask = (jnp.arange(BLOCK, dtype=jnp.int32)[None, :] < own_live[:, None]).reshape(
        own_rows, 1
    )
    return jnp.where(live_mask, total, 0.0).astype(jnp.bfloat16)


def solution(mesh):
    in_specs = (
        P("gx", "gy"),
        P("gy", ("gz", "gx")),
        P(None, None, "gy"),
        P("gx", None, "gz"),
        P("gx"),
        P("gx"),
    )
    out_specs = P(("gx", "gy"), "gz")
    return jax.shard_map(body, mesh=mesh, in_specs=in_specs, out_specs=out_specs, check_vma=False)
```

profile of v0, /device:TPU:1, one launch (start us, length us, event | category | flops | bytes accessed | tf_op | source)
XLA Modules:
  0.0 278.8 jit_solution(411881308684127946)
XLA Ops:
  6.5 0.0 copy-start
  6.5 0.0 all-gather.3.cloned.1.call-start
  6.5 0.7 all-gather.3.cloned.1.call-update
  7.3 0.0 all-gather.5.cloned.1.call-start
  7.3 0.7 all-gather.5.cloned.1.call-update
  8.0 2.2 copy.8
  10.2 0.5 convolution_convert_fusion
  10.7 0.4 convolution_bitcast_fusion
  11.2 0.7 broadcast_in_dim.11
  11.8 5.0 %all-to-all-start.1 = ((f32[4,4,128,16]{2,3,1,0:T(8,128)}), f32[4,4,128,16]{2,3,1,0:T(8,128)S(1)}, u32[]{:S(2)}, u32[]{:S(2)}) async-start(f32[4,4,128,16]{2,3,1,0:T(8,128)} %broadcast_in_dim.11), calls=%async_computation.1 | async-start | bytes 262144 | tf_op jit(solution)/shard_map/all_to_all | solution.py:12
  16.9 120.7 %all-gather.3.cloned.1.call-done = bf16[1152,4608]{0,1:T(8,128)(2,1)} async-done(((bf16[1152,288]{0,1:T(8,128)(2,1)}), bf16[1152,4608]{0,1:T(8,128)(2,1)}) %all-gather.3.cloned.1.call-update) | async-done | bytes 10616848 | tf_op jit(solution)/shard_map/all_gather | solution.py:75
  137.5 11.9 %convolution_convert_fusion.1 = bf16[512,4608]{1,0:T(8,128)(2,1)} fusion(bf16[512,1152]{1,0:T(8,128)(2,1)S(1)} %copy-done, bf16[1152,4608]{0,1:T(8,128)(2,1)} %all-gather.3.cloned.1.call-done), kind=kOutput, calls=%fused_computation.2 | convolution fusion | flops 5438177280 | bytes 16515072 | tf_op jit(solution)/shard_map/dot_general | solution.py:73
  149.5 0.0 all-to-all-done.1
  149.5 5.3 %all-to-all-start = ((bf16[4,128,4608]{2,1,0:T(8,128)(2,1)}), bf16[4,128,4608]{2,1,0:T(8,128)(2,1)}, u32[]{:S(2)}, u32[]{:S(2)}) async-start(bf16[4,128,4608]{2,1,0:T(8,128)(2,1)} %bitcast.31), calls=%async_computation | async-start | bytes 9437184 | tf_op jit(solution)/shard_map/all_to_all | solution.py:28
  154.7 0.6 dynamic_slice.9
  155.3 0.6 iota_compare_fusion.1
  156.0 0.1 iota_compare_fusion
  156.1 92.9 %all-gather.5.cloned.1.call-done = bf16[64,16,4608]{2,1,0:T(8,128)(2,1)} async-done(((bf16[4,16,4608]{2,1,0:T(8,128)(2,1)}), bf16[64,16,4608]{2,1,0:T(8,128)(2,1)}) %all-gather.5.cloned.1.call-update) | async-done | bytes 9437200 | tf_op jit(solution)/shard_map/all_gather | solution.py:62
  249.0 12.8 %copy.10 = bf16[8,8,16,4608]{3,1,2,0:T(8,128)(2,1)} copy(bf16[8,8,16,4608]{3,2,1,0:T(8,128)(2,1)} %bitcast.29) | data formatting | bytes 18874368
  261.8 5.1 %fusion.7 = f32[1,73728]{1,0:T(1,128)S(1)} fusion(bf16[64,73728]{1,0:T(8,128)(2,1)} %bitcast.28, pred[4,64]{1,0:T(4,128)(4,1)S(1)} %iota_compare_fusion, s32[]{:T(128)S(6)} %select_n.9), kind=kOutput, calls=%fused_computation.13 | convolution fusion | flops 9437184 | bytes 9732356 | tf_op jit(solution)/shard_map/dot_general | solution.py:65
  266.9 0.2 reshape.51
  267.1 0.0 all-to-all-done
  267.1 3.3 %convert_reduce_fusion = f32[128,4608]{1,0:T(8,128)S(1)} fusion(bf16[4,128,4608]{2,1,0:T(8,128)(2,1)} %all-to-all-done), kind=kLoop, calls=%fused_computation.1 | loop fusion | flops 4128768 | bytes 7077888 | tf_op jit(solution)/shard_map/reduce_sum | solution.py:29
  270.4 1.5 fusion.2
  (7 shorter events, 0.0 us)
Async XLA Ops:
  6.5 4.2 %copy-start = (bf16[512,1152]{1,0:T(8,128)(2,1)S(1)}, bf16[512,1152]{1,0:T(8,128)(2,1)}, u32[]{:S(2)}) copy-start(bf16[512,1152]{1,0:T(8,128)(2,1)} %param.6) | copy-start | bytes 3538948
  6.5 131.0 %all-gather.3.cloned.1.call-start = ((), (), s32[]{:S(2)}) async-start(), calls=%async_computation.2 | async-start | bytes 11280384 | tf_op jit(solution)/shard_map/all_gather | solution.py:75
  7.3 241.8 %all-gather.5.cloned.1.call-start = ((), (), s32[]{:S(2)}) async-start(), calls=%async_computation.3 | async-start | bytes 10027008 | tf_op jit(solution)/shard_map/all_gather | solution.py:62
  8.0 2.2 copy-start.1
  11.8 137.6 %all-to-all-start.1 = ((f32[4,4,128,16]{2,3,1,0:T(8,128)}), f32[4,4,128,16]{2,3,1,0:T(8,128)S(1)}, u32[]{:S(2)}, u32[]{:S(2)}) async-start(f32[4,4,128,16]{2,3,1,0:T(8,128)} %broadcast_in_dim.11), calls=%async_computation.1 | async-start | bytes 262144 | tf_op jit(solution)/shard_map/all_to_all | solution.py:12
  149.5 5.3 %copy-start.2 = (s32[4]{0:T(128)S(1)}, s32[4]{0:T(128)}, u32[]{:S(2)}) copy-start(s32[4]{0:T(128)} %param.11) | copy-start | bytes 52
  149.5 117.6 %all-to-all-start = ((bf16[4,128,4608]{2,1,0:T(8,128)(2,1)}), bf16[4,128,4608]{2,1,0:T(8,128)(2,1)}, u32[]{:S(2)}, u32[]{:S(2)}) async-start(bf16[4,128,4608]{2,1,0:T(8,128)(2,1)} %bitcast.31), calls=%async_computation | async-start | bytes 9437184 | tf_op jit(solution)/shard_map/all_to_all | solution.py:28
Sparse Core Ops, SparseCore 0:
  9.1 128.3 all-gather.2
  139.3 109.6 all-gather.4
where the time goes:
time: 279 us
  waiting for transfers between devices  215 us (77%)
  matrix products  19.4 us (7%)
  local copies, waits for them, and re-layouts  16.5 us (6%)
  between operations  13.5 us (5%)
  starting transfers between devices  10.3 us (4%)
  other arithmetic  4.06 us (1%)
    all_gather x1, waiting for transfers between devices, body(): lax.all_gather(base_up_weight, 'gx', axis=1, tiled=True)  121 us
    all_gather x1, waiting for transfers between devices, body(): lax.all_gather(adapter_up_weight, 'gx', axis=0, tiled=True)  92.9 us
    unnamed x8, local copies, waits for them, and re-layouts  15 us
    dot_general x1, matrix products, body(): jnp.dot(tokens, lax.all_gather(base_up_weight, 'gx', axis=1, tiled=True),...  11.9 us
  transfers between devices with their start and end apart: 4, of which 2 were waited for; matrix products, arithmetic and copies ran while one was open for 13% of the time, Pallas kernels for 0%

commit v1 on v0

--- a/solution.py
+++ b/solution.py
@@ -72,7 +72,9 @@
     expand = expand.reshape(own_rows, out_width)
     partial_value = jnp.dot(
         tokens,
-        lax.all_gather(base_up_weight, "gx", axis=1, tiled=True),
+        jnp.concatenate(
+            lax.all_to_all(jnp.stack([base_up_weight] * lax.axis_size("gx")), "gx", 0, 0), axis=1
+        ),
         preferred_element_type=jnp.float32,
     )
     extra = 2.0 * expand

time: 279 us -> 440 us (1.58)
  the two profiles are of different devices: /device:TPU:1 before, /device:TPU:166 now
where the time goes in v1:
time: 440 us
  waiting for transfers between devices  366 us (83%)
  local copies, waits for them, and re-layouts  20.6 us (5%)
  matrix products  19.3 us (4%)
  starting transfers between devices  16.1 us (4%)
  between operations  13.5 us (3%)
    all_to_all x1, waiting for transfers between devices, body(): lax.all_to_all(jnp.stack([base_up_weight] * lax.axis_size('gx')), 'gx', 0...  331 us
    all_to_all x1, waiting for transfers between devices, summed_on_arrival(): tiles = lax.all_to_all(in_blocks(array, dim, size), axis, 0, 0, tiled=True)  34.5 us
    unnamed x10, local copies, waits for them, and re-layouts  13.3 us
    dot_general x1, matrix products, body(): jnp.dot(tokens, jnp.concatenate(lax.all_to_all(jnp.stack([base_up_weight]...  11.9 us
  transfers between devices with their start and end apart: 4, of which 2 were waited for; matrix products, arithmetic and copies ran while one was open for 8% of the time, Pallas kernels for 0%

profile of v1, /device:TPU:166, one launch (start us, length us, event | category | flops | bytes accessed | tf_op | source)
XLA Modules:
  0.0 439.5 jit_solution(264797240698646366)
XLA Ops:
  6.5 5.8 %stack.2 = bf16[16,1152,288]{1,2,0:T(8,128)(2,1)} broadcast(bf16[1152,288]{0,1:T(8,128)(2,1)} %param.7), dimensions={1,2} | broadcast | bytes 11280384 | tf_op jit(solution)/shard_map/stack | solution.py:76
  12.4 6.7 %all-to-all-start = ((bf16[16,1152,288]{1,2,0:T(8,128)(2,1)}), bf16[16,1152,288]{1,2,0:T(8,128)(2,1)}, u32[]{:S(2)}, u32[]{:S(2)}) async-start(bf16[16,1152,288]{1,2,0:T(8,128)(2,1)} %stack.2), calls=%async_computation | async-start | bytes 21233664 | tf_op jit(solution)/shard_map/all_to_all | solution.py:76
  19.1 0.0 all-gather.2.cloned.1.call-start
  19.1 0.7 all-gather.2.cloned.1.call-update
  19.8 0.0 copy-start.2
  19.9 0.5 copy.10
  20.4 0.1 copy-done.2
  20.5 0.5 convolution_convert_fusion
  21.0 0.4 convolution_bitcast_fusion
  21.4 330.8 %all-to-all-done = bf16[16,1152,288]{1,2,0:T(8,128)(2,1)} async-done(((bf16[16,1152,288]{1,2,0:T(8,128)(2,1)}), bf16[16,1152,288]{1,2,0:T(8,128)(2,1)}, u32[]{:S(2)}, u32[]{:S(2)}) %all-to-all-start) | async-done | bytes 10616864 | tf_op jit(solution)/shard_map/all_to_all | solution.py:76
  352.2 0.7 broadcast_in_dim.11
  352.9 4.0 all-to-all-start.2
  356.9 11.9 %convolution_convert_fusion.1 = bf16[512,4608]{1,0:T(8,128)(2,1)} fusion(bf16[512,1152]{1,0:T(8,128)(2,1)S(1)} %copy-done, bf16[1152,4608]{0,1:T(8,128)(2,1)} %bitcast.2), kind=kOutput, calls=%fused_computation.2 | convolution fusion | flops 5438177280 | bytes 16515072 | tf_op jit(solution)/shard_map/dot_general | solution.py:73
  368.8 5.3 %all-to-all-start.1 = ((bf16[4,128,4608]{2,1,0:T(8,128)(2,1)}), bf16[4,128,4608]{2,1,0:T(8,128)(2,1)}, u32[]{:S(2)}, u32[]{:S(2)}) async-start(bf16[4,128,4608]{2,1,0:T(8,128)(2,1)} %bitcast.34), calls=%async_computation.1 | async-start | bytes 9437184 | tf_op jit(solution)/shard_map/all_to_all | solution.py:28
  374.1 0.6 dynamic_slice.9
  374.7 0.6 iota_compare_fusion.1
  375.4 0.1 iota_compare_fusion
  375.4 0.0 all-gather.2.cloned.1.call-done
  375.5 12.7 %copy.12 = bf16[8,8,16,4608]{3,1,2,0:T(8,128)(2,1)} copy(bf16[8,8,16,4608]{3,2,1,0:T(8,128)(2,1)} %bitcast.32) | data formatting | bytes 18874368
  388.2 5.0 %fusion.7 = f32[1,73728]{1,0:T(1,128)S(1)} fusion(bf16[64,73728]{1,0:T(8,128)(2,1)} %bitcast.31, pred[4,64]{1,0:T(4,128)(4,1)S(1)} %iota_compare_fusion, s32[]{:T(128)S(6)} %select_n.9), kind=kOutput, calls=%fused_computation.13 | convolution fusion | flops 9437184 | bytes 9732356 | tf_op jit(solution)/shard_map/dot_general | solution.py:65
  393.2 0.2 reshape.61
  393.4 34.5 %all-to-all-done.1 = bf16[4,128,4608]{2,1,0:T(8,128)(2,1)} async-done(((bf16[4,128,4608]{2,1,0:T(8,128)(2,1)}), bf16[4,128,4608]{2,1,0:T(8,128)(2,1)}, u32[]{:S(2)}, u32[]{:S(2)}) %all-to-all-start.1) | async-done | bytes 4718624 | tf_op jit(solution)/shard_map/all_to_all | solution.py:28
  427.9 3.3 convert_reduce_fusion
  431.2 1.5 fusion.2
  (9 shorter events, 0.0 us)
Async XLA Ops:
  6.5 14.4 %copy-start = (bf16[512,1152]{1,0:T(8,128)(2,1)S(1)}, bf16[512,1152]{1,0:T(8,128)(2,1)}, u32[]{:S(2)}) copy-start(bf16[512,1152]{1,0:T(8,128)(2,1)} %param.6) | copy-start | bytes 3538948
  12.4 7.5 %copy-start.1 = (bf16[64,16,1152]{2,1,0:T(8,128)(2,1)S(1)}, bf16[64,16,1152]{2,1,0:T(8,128)(2,1)}, u32[]{:S(2)}) copy-start(bf16[64,16,1152]{2,1,0:T(8,128)(2,1)} %param.8) | copy-start | bytes 7077892
  12.4 339.8 %all-to-all-start = ((bf16[16,1152,288]{1,2,0:T(8,128)(2,1)}), bf16[16,1152,288]{1,2,0:T(8,128)(2,1)}, u32[]{:S(2)}, u32[]{:S(2)}) async-start(bf16[16,1152,288]{1,2,0:T(8,128)(2,1)} %stack.2), calls=%async_computation | async-start | bytes 21233664 | tf_op jit(solution)/shard_map/all_to_all | solution.py:76
  19.1 356.4 %all-gather.2.cloned.1.call-start = ((), (), s32[]{:S(2)}) async-start(), calls=%async_computation.3 | async-start | bytes 10027008 | tf_op jit(solution)/shard_map/all_gather | solution.py:62
  19.8 0.7 copy-start.2
  352.9 15.9 %all-to-all-start.2 = ((f32[4,4,128,16]{2,3,1,0:T(8,128)}), f32[4,4,128,16]{2,3,1,0:T(8,128)S(1)}, u32[]{:S(2)}, u32[]{:S(2)}) async-start(f32[4,4,128,16]{2,3,1,0:T(8,128)} %broadcast_in_dim.11), calls=%async_computation.2 | async-start | bytes 262144 | tf_op jit(solution)/shard_map/all_to_all | solution.py:12
  368.8 5.3 %copy-start.3 = (s32[4]{0:T(128)S(1)}, s32[4]{0:T(128)}, u32[]{:S(2)}) copy-start(s32[4]{0:T(128)} %param.11) | copy-start | bytes 52
  368.8 59.1 %all-to-all-start.1 = ((bf16[4,128,4608]{2,1,0:T(8,128)(2,1)}), bf16[4,128,4608]{2,1,0:T(8,128)(2,1)}, u32[]{:S(2)}, u32[]{:S(2)}) async-start(bf16[4,128,4608]{2,1,0:T(8,128)(2,1)} %bitcast.34), calls=%async_computation.1 | async-start | bytes 9437184 | tf_op jit(solution)/shard_map/all_to_all | solution.py:28
Sparse Core Ops, SparseCore 0:
  21.7 323.3 all-gather.1
